TPU v7x, 32 devices: a whole 2x2x4 slice. The times are simulated.
32 devices in a mesh: gx: 4 (over z), gy: 4 (over y, x), gz: 2 (over core).
Axes of the slice: x: 2, y: 2, z: 4, core: 2. Of those that a mesh axis runs over, the one named last changes fastest.
Arguments:
- east_wind: float32 [96, 512, 512], P('gz', 'gx', 'gy'), may hold values from -6 to 6
- north_wind: float32 [96, 512, 512], P('gz', 'gx', 'gy'), may hold values from -6 to 6
- vertical_wind: float32 [96, 512, 512], P('gz', 'gx', 'gy'), may hold values from -6 to 6
- geopotential: float32 [96, 512, 512], P('gz', 'gx', 'gy'), may hold values from -6 to 6
- pressure: float32 [96, 512, 512], P('gz', 'gx', 'gy'), may hold values from -6 to 6
- column_mass: float32 [512, 512], P('gx', 'gy'), may hold values from 0.5 to 2
Outputs:
- east_after: float32 [96, 512, 512], P('gz', 'gx', 'gy')
- north_after: float32 [96, 512, 512], P('gz', 'gx', 'gy')
- vertical_after: float32 [96, 512, 512], P('gz', 'gx', 'gy')
- geo_after: float32 [96, 512, 512], P('gz', 'gx', 'gy')
- pressure_after: float32 [96, 512, 512], P('gz', 'gx', 'gy')
All inputs are finite; a program needn't handle non-finite values.
Results may differ from a plain program's by a relative error of at most 0.0003.
Values sent between devices are 32-bit elements; how exact they have to be, the bound alone decides.
A program may use at most 128 MiB of HBM per device.

v0:
```python
import functools

import jax
import jax.numpy as jnp
from jax import lax
from jax.experimental import pallas as pl
from jax.experimental.pallas import tpu as pltpu
from jax.sharding import PartitionSpec as P

ITERS = 3
STIFF = 30.0
PAD = 8
ROWS = 16
UNROLL = 4


def roll(value, shift):
    if isinstance(shift, int):
        shift = shift % value.shape[1]
    return pltpu.roll(value, shift, 1)


def kernel(n, ni, nj, sizes, east_in, north_in, vert_in, geo_in, press_in, mass,
           east, north, vert, geo, press,
           pp, up, psum, dvg, mu_s, c_s, planes, bounds,
           row_out, row_in, col_out, col_in, z_out, z_in,
           load_sem, row_send, row_recv, col_send, col_recv, z_send, z_recv):
    nx, ny, nz = sizes
    ix, iy, iz = lax.axis_index("gx"), lax.axis_index("gy"), lax.axis_index("gz")
    xs = (lax.rem(ix + nx - 1, nx), lax.rem(ix + 1, nx))
    ys = (lax.rem(iy + ny - 1, ny), lax.rem(iy + 1, ny))

    loads = [
        pltpu.make_async_copy(press_in, pp.at[:, pl.ds(PAD, ni), :], load_sem.at[0]),
        pltpu.make_async_copy(east_in, up.at[:, pl.ds(PAD, ni), :], load_sem.at[1]),
        pltpu.make_async_copy(north_in, north, load_sem.at[2]),
        pltpu.make_async_copy(vert_in, vert, load_sem.at[3]),
        pltpu.make_async_copy(geo_in, geo, load_sem.at[4]),
    ]
    for load in loads:
        load.start()

    barrier = pltpu.get_barrier_semaphore()
    for t in range(2):
        pl.semaphore_signal(barrier, inc=1, device_id={"gx": xs[t]})
        pl.semaphore_signal(barrier, inc=1, device_id={"gy": ys[t]})
    for d in range(1, nz):
        pl.semaphore_signal(barrier, inc=1, device_id={"gz": lax.rem(iz + d, nz)})
    pl.semaphore_wait(barrier, 4 + nz - 1)

    def row_copy(slot, t):
        return pltpu.make_async_remote_copy(
            src_ref=row_out.at[slot, t], dst_ref=row_in.at[slot, 1 - t],
            send_sem=row_send.at[slot, t], recv_sem=row_recv.at[slot, 1 - t],
            device_id={"gx": xs[t]})

    def col_copy(slot, t):
        return pltpu.make_async_remote_copy(
            src_ref=col_out.at[slot, t], dst_ref=col_in.at[slot, 1 - t],
            send_sem=col_send.at[slot, t], recv_sem=col_recv.at[slot, 1 - t],
            device_id={"gy": ys[t]})

    def z_copy(slot, d):
        return pltpu.make_async_remote_copy(
            src_ref=z_out.at[slot], dst_ref=z_in.at[slot, d - 1],
            send_sem=z_send.at[slot, d - 1], recv_sem=z_recv.at[slot, d - 1],
            device_id={"gz": lax.rem(iz + d, nz)})

    lane = lax.broadcasted_iota(jnp.int32, (ROWS, nj), 1)
    pair = lane // 2

    def send_rows(slot, ref):
        row_out[slot, 0] = ref[:, PAD : PAD + 2, :]
        row_out[slot, 1] = ref[:, PAD + ni - 2 : PAD + ni, :]
        for t in range(2):
            row_copy(slot, t).start()

    def recv_rows(slot, ref):
        for t in range(2):
            row_copy(slot, t).wait()
        ref[:, PAD - 2 : PAD, :] = row_in[slot, 0]
        ref[:, PAD + ni : PAD + ni + 2, :] = row_in[slot, 1]

    def packed(value, k, packs):
        turned = roll(value, 2 * k + 2)
        return (jnp.where(pair == k + 1, turned, packs[0]), jnp.where(pair == k, turned, packs[1]))

    def strips(body):
        @pl.loop(0, ni // ROWS)
        def _(s):
            body(pl.multiple_of(s * ROWS, ROWS))

    def send_cols(slot, load_level):
        def body(r0):
            zero = jnp.zeros((ROWS, nj), jnp.float32)

            def group(q, packs):
                for e in range(UNROLL):
                    k = q * UNROLL + e
                    packs = packed(load_level(k, r0), k, packs)
                return packs

            packs = lax.fori_loop(0, n // UNROLL, group, (zero, zero))
            for t in range(2):
                col_out[slot, t, pl.ds(r0, ROWS), :] = packs[t]

        strips(body)
        for t in range(2):
            col_copy(slot, t).start()

    loads[0].wait()
    send_rows(0, pp)
    send_cols(0, lambda k, r0: pp[k, pl.ds(PAD + r0, ROWS), :])
    loads[1].wait()
    send_rows(ITERS, up)
    loads[2].wait()
    send_cols(ITERS, lambda k, r0: north[k, pl.ds(r0, ROWS), :])

    stiff = STIFF * mass[...]
    root = jnp.sqrt(1.0 + 4.0 * stiff)
    major = 0.5 * (1.0 + 2.0 * stiff + root)
    mu_s[...] = stiff / major
    c_s[...] = 1.0 / major
    planes[0] = jnp.log(stiff / major)
    planes[1] = major / root
    planes[2] = major / stiff

    recv_rows(0, pp)
    recv_rows(ITERS, up)
    for slot in (0, ITERS):
        for t in range(2):
            col_copy(slot, t).wait()
    loads[3].wait()
    loads[4].wait()

    def pass_one(it):
        def body(r0):
            rows = pl.ds(r0, ROWS)
            m, mu, c = mass[rows, :], mu_s[rows, :], c_s[rows, :]
            weak, strong = 0.05 * m, 0.2 * m
            left, right = col_in[it, 0, rows, :], col_in[it, 1, rows, :]
            if it == 0:
                vleft, vright = col_in[ITERS, 0, rows, :], col_in[ITERS, 1, rows, :]

            def star(k):
                at = pl.ds(PAD + r0, ROWS)
                p = pp[k, at, :]
                low = jnp.where(lane < 2, roll(left, (2 * nj - 2 * k) if isinstance(k, int) else nj - 2 * k), roll(p, 2))
                high = jnp.where(lane >= nj - 2, roll(right, nj - 4 - 2 * k), roll(p, nj - 2))
                total = (pp[k, pl.ds(PAD + r0 + 2, ROWS), :] + pp[k, pl.ds(PAD + r0 - 2, ROWS), :]) + (low + high) - 4.0 * p
                if it == 0:
                    v = north[k, rows, :]
                    vlow = jnp.where(lane < 1, roll(vleft, nj - 1 - 2 * k), roll(v, 1))
                    vhigh = jnp.where(lane >= nj - 1, roll(vright, nj - 3 - 2 * k), roll(v, nj - 1))
                    d = strong * (up[k, pl.ds(PAD + r0 + 1, ROWS), :] - up[k, pl.ds(PAD + r0 - 1, ROWS), :] + (vhigh - vlow))
                    psum[k, at, :] = p
                else:
                    d = dvg[k, rows, :]
                    psum[k, at, :] = psum[k, at, :] + p
                d = d - weak * total
                if it < ITERS - 1:
                    dvg[k, rows, :] = d
                ps = p - d
                press[k, rows, :] = ps
                return ps

            def sweep(k, above, below, state):
                y, dn, weight = state
                f = c * (vert[k, rows, :] + 0.5 * geo[k, rows, :] - (above - below))
                y = mu * y + f
                vert[k, rows, :] = y
                return y, dn + weight * f, weight * mu

            def steps(ks, carry):
                older, newer, state = carry
                for k in ks:
                    ps = star(k)
                    if not (isinstance(k, int) and k == 0):
                        state = sweep(k - 1, ps, older, state)
                    older, newer = newer, ps
                return older, newer, state

            zero = jnp.zeros((ROWS, nj), jnp.float32)
            carry = (zero, zero, (zero, zero, zero + 1.0))
            carry = steps(range(UNROLL), carry)
            planes_lo = press[0, rows, :]

            def group(q, carry):
                return steps([q * UNROLL + e for e in range(UNROLL)], carry)

            older, newer, state = lax.fori_loop(1, n // UNROLL, group, carry)
            y, dn, _ = sweep(n - 1, zero, older, state)
            z_out[it, 0, rows, :] = y
            z_out[it, 1, rows, :] = dn
            z_out[it, 2, rows, :] = c * planes_lo
            z_out[it, 3, rows, :] = c * newer

        strips(body)

    def interface(it):
        def body(r0):
            rows = pl.ds(r0, ROWS)
            mu, logmu, kappa, inv = mu_s[rows, :], planes[0, rows, :], planes[1, rows, :], planes[2, rows, :]
            zero = jnp.zeros((ROWS, nj), jnp.float32)

            def power(m):
                if not isinstance(m, int):
                    m = jnp.maximum(m, 0).astype(jnp.float32)
                return jnp.exp(m * logmu)

            near = power(n - 1)
            below, above, to_low, to_high = zero, zero, zero, zero
            pieces = {}

            def piece(d, which):
                if abs(d) >= nz:
                    return zero
                if d == 0:
                    return z_out[it, which, rows, :]
                value = z_in[it, (nz - d - 1) % nz if d > 0 else -d - 1, which, rows, :]
                inside = jnp.logical_and(iz + d >= 0, iz + d < nz)
                return jnp.where(inside, value, 0.0)

            own_up = own_dn = zero
            for d in range(-(nz - 1), nz):
                j = iz + d
                inside = jnp.logical_and(j >= 0, j < nz)
                under, over = piece(d - 1, 3), piece(d + 1, 2)
                upt = piece(d, 0) + near * under - over
                dnt = piece(d, 1) + under - near * over
                if d == 0:
                    own_up, own_dn = upt, dnt
                    delta_low, delta_high = under, over
                elif d < 0:
                    below = below + jnp.where(inside, power(n * (-1 - d)) * upt, 0.0)
                else:
                    above = above + jnp.where(inside, power(n * (d - 1)) * dnt, 0.0)
                to_low = to_low + jnp.where(inside, power(n * j + 1) * dnt, 0.0)
                to_high = to_high + jnp.where(inside, power(n * (nz - 1 - j) + 1) * upt, 0.0)
            q = power(n * nz + 1)
            scale = kappa / (1.0 - q * q)
            alpha = kappa * below + (q * to_high - to_low) * scale * power(n * iz)
            beta = kappa * above + (q * to_low - to_high) * scale * power(n * (nz - 1 - iz))
            far = power(n + 1)
            bounds[2, rows, :] = kappa * mu * own_dn + alpha + beta * far
            bounds[3, rows, :] = kappa * mu * own_up + beta + alpha * far
            alpha = alpha + kappa * delta_low * inv
            beta = beta - kappa * delta_high * inv
            bounds[0, rows, :] = kappa * mu * z_out[it, 0, rows, :] + beta
            bounds[1, rows, :] = alpha * power(n)

        strips(body)

    def pass_two(it):
        last = it == ITERS - 1

        def body(r0):
            rows = pl.ds(r0, ROWS)
            mu, inv = mu_s[rows, :], planes[2, rows, :]
            half = 0.5 * mass[rows, :]
            zero = jnp.zeros((ROWS, nj), jnp.float32)

            def finish(k, above, below, packs):
                p = press[k, rows, :] - half * (above - below)
                if last:
                    press[k, rows, :] = p
                    return packs
                pp[k, pl.ds(PAD + r0, ROWS), :] = p
                return packed(p, k, packs)

            def steps(ks, carry):
                x, h, older, newer, packs = carry
                for k in ks:
                    x = mu * x + vert[k, rows, :]
                    v = x + h
                    h = h * inv
                    vert[k, rows, :] = v
                    geo[k, rows, :] = geo[k, rows, :] + 0.5 * v
                    if not (isinstance(k, int) and k == n - 1):
                        packs = finish(k + 1, older, v, packs)
                    older, newer = newer, v
                return x, h, older, newer, packs

            top = bounds[3, rows, :]
            carry = (bounds[0, rows, :], bounds[1, rows, :], zero, top, (zero, zero))
            carry = steps([n - 1 - e for e in range(UNROLL)], carry)

            def group(q, carry):
                return steps([n - 1 - q * UNROLL - e for e in range(UNROLL)], carry)

            _, _, older, newer, packs = lax.fori_loop(1, n // UNROLL, group, carry)
            packs = finish(0, older, bounds[2, rows, :], packs)
            if not last:
                for t in range(2):
                    col_out[it + 1, t, rows, :] = packs[t]

        strips(body)

    def winds():
        def body(r0):
            rows = pl.ds(r0, ROWS)
            left = col_in[0, 0, rows, :]
            right = col_in[0, 1, rows, :]
            for it in range(1, ITERS):
                left = left + col_in[it, 0, rows, :]
                right = right + col_in[it, 1, rows, :]

            def group(q, carry):
                for e in range(UNROLL):
                    k = q * UNROLL + e
                    at = pl.ds(PAD + r0, ROWS)
                    p = psum[k, at, :]
                    east[k, rows, :] = up[k, at, :] - 0.25 * (
                        psum[k, pl.ds(PAD + r0 + 1, ROWS), :] - psum[k, pl.ds(PAD + r0 - 1, ROWS), :])
                    low = jnp.where(lane < 1, roll(left, nj - 1 - 2 * k), roll(p, 1))
                    high = jnp.where(lane >= nj - 1, roll(right, nj - 3 - 2 * k), roll(p, nj - 1))
                    north[k, rows, :] = north[k, rows, :] - 0.25 * (high - low)
                return carry

            lax.fori_loop(0, n // UNROLL, group, 0)

        strips(body)

    for it in range(ITERS):
        if it > 0:
            recv_rows(it, pp)
            for t in range(2):
                col_copy(it, t).wait()
        pass_one(it)
        for d in range(1, nz):
            z_copy(it, d).start()
        if it == ITERS - 1:
            for t, at in ((0, PAD - 2), (1, PAD + ni)):
                total = row_in[0, t]
                for slot in range(1, ITERS):
                    total = total + row_in[slot, t]
                psum[:, at : at + 2, :] = total
            winds()
        for d in range(1, nz):
            z_copy(it, d).wait()
        interface(it)
        pass_two(it)
        if it < ITERS - 1:
            send_rows(it + 1, pp)
            for t in range(2):
                col_copy(it + 1, t).start()


def local(sizes, east, north, vert, geo, press, mass):
    n, ni, nj = east.shape
    nz = sizes[2]
    f32 = jnp.float32
    slots = ITERS + 1
    field = pltpu.VMEM((n, ni, nj), f32)
    padded = pltpu.VMEM((n, ni + 2 * PAD, nj), f32)
    plane = pltpu.VMEM((ni, nj), f32)
    return pl.pallas_call(
        functools.partial(kernel, n, ni, nj, sizes),
        out_shape=[jax.ShapeDtypeStruct((n, ni, nj), f32)] * 5,
        in_specs=[pl.BlockSpec(memory_space=pl.ANY)] * 5 + [pl.BlockSpec(memory_space=pltpu.VMEM)],
        out_specs=[pl.BlockSpec(memory_space=pltpu.VMEM)] * 5,
        scratch_shapes=[
            padded, padded, padded, field, plane, plane,
            pltpu.VMEM((3, ni, nj), f32),
            pltpu.VMEM((4, ni, nj), f32),
            pltpu.VMEM((slots, 2, n, 2, nj), f32),
            pltpu.VMEM((slots, 2, n, 2, nj), f32),
            pltpu.VMEM((slots, 2, ni, nj), f32),
            pltpu.VMEM((slots, 2, ni, nj), f32),
            pltpu.VMEM((ITERS, 4, ni, nj), f32),
            pltpu.VMEM((ITERS, nz - 1, 4, ni, nj), f32),
            pltpu.SemaphoreType.DMA((5,)),
            pltpu.SemaphoreType.DMA((slots, 2)),
            pltpu.SemaphoreType.DMA((slots, 2)),
            pltpu.SemaphoreType.DMA((slots, 2)),
            pltpu.SemaphoreType.DMA((slots, 2)),
            pltpu.SemaphoreType.DMA((ITERS, nz - 1)),
            pltpu.SemaphoreType.DMA((ITERS, nz - 1)),
        ],
        compiler_params=pltpu.CompilerParams(
            collective_id=0, has_side_effects=True, vmem_limit_bytes=60 * 1024 * 1024),
    )(east, north, vert, geo, press, mass)


def solution(mesh):
    sizes = (mesh.shape["gx"], mesh.shape["gy"], mesh.shape["gz"])
    cube = P("gz", "gx", "gy")
    return jax.shard_map(
        functools.partial(local, sizes), mesh=mesh,
        in_specs=(cube,) * 5 + (P("gx", "gy"),), out_specs=(cube,) * 5, check_vma=False)
```

profile of v0, /device:TPU:0, one launch (start us, length us, event | category | flops | bytes accessed | tf_op | source)
XLA Modules:
  0.0 129.0 jit_solution(1678642506585930556)
XLA Ops:
  0.6 113.6 %shard_map.101 = (f32[48,128,128]{2,1,0:T(8,128)}, f32[48,128,128]{2,1,0:T(8,128)}, f32[48,128,128]{2,1,0:T(8,128)}, f32[48,128,128]{2,1,0:T(8,128)}, f32[48,128,128]{2,1,0:T(8,128)}) custom-call(f32[48,128,128]{2,1,0:T(8,128)} %east_in.1, f32[48,128,128]{2,1,0:T(8,128)} %north_in.1, f32[48,128,128]{2,1,0:T(8,128)} %vert_in.1, f32[48,128,128]{2,1,0:T(8,128)} %geo_in.1, ...), custom_call_target="tpu_custom_call" | custom-call | tf_op jit(solution)/shard_map/pallas_call | solution.py:357
  114.2 0.0 copy-start.3
  114.2 4.1 %copy.16 = f32[48,128,128]{2,1,0:T(8,128)} copy(f32[48,128,128]{2,1,0:T(8,128)} %get-tuple-element.10) | data formatting | bytes 6291456
  118.3 0.0 copy-done.3
  118.3 0.0 copy-start.2
  118.3 1.7 %copy.17 = f32[48,128,128]{2,1,0:T(8,128)} copy(f32[48,128,128]{2,1,0:T(8,128)S(1)} %copy-done.3) | data formatting | bytes 6291456
  120.0 1.4 %copy-done.2 = f32[48,128,128]{2,1,0:T(8,128)S(1)} copy-done((f32[48,128,128]{2,1,0:T(8,128)S(1)}, f32[48,128,128]{2,1,0:T(8,128)}, u32[]{:S(2)}) %copy-start.2) | copy-done | bytes 3145752
  121.3 0.0 copy-start.1
  121.3 1.7 %copy.18 = f32[48,128,128]{2,1,0:T(8,128)} copy(f32[48,128,128]{2,1,0:T(8,128)S(1)} %copy-done.2) | data formatting | bytes 6291456
  123.0 1.4 %copy-done.1 = f32[48,128,128]{2,1,0:T(8,128)S(1)} copy-done((f32[48,128,128]{2,1,0:T(8,128)S(1)}, f32[48,128,128]{2,1,0:T(8,128)}, u32[]{:S(2)}) %copy-start.1) | copy-done | bytes 3145752
  124.3 0.0 copy-start
  124.3 1.7 %copy.19 = f32[48,128,128]{2,1,0:T(8,128)} copy(f32[48,128,128]{2,1,0:T(8,128)S(1)} %copy-done.1) | data formatting | bytes 6291456
  126.0 1.4 %copy-done = f32[48,128,128]{2,1,0:T(8,128)S(1)} copy-done((f32[48,128,128]{2,1,0:T(8,128)S(1)}, f32[48,128,128]{2,1,0:T(8,128)}, u32[]{:S(2)}) %copy-start) | copy-done | bytes 3145752
  127.4 1.7 %copy.20 = f32[48,128,128]{2,1,0:T(8,128)} copy(f32[48,128,128]{2,1,0:T(8,128)S(1)} %copy-done) | data formatting | bytes 6291456
Async XLA Ops:
  114.2 4.1 %copy-start.3 = (f32[48,128,128]{2,1,0:T(8,128)S(1)}, f32[48,128,128]{2,1,0:T(8,128)}, u32[]{:S(2)}) copy-start(f32[48,128,128]{2,1,0:T(8,128)} %get-tuple-element.11) | copy-start | bytes 9437188
  118.3 3.0 %copy-start.2 = (f32[48,128,128]{2,1,0:T(8,128)S(1)}, f32[48,128,128]{2,1,0:T(8,128)}, u32[]{:S(2)}) copy-start(f32[48,128,128]{2,1,0:T(8,128)} %get-tuple-element.12) | copy-start | bytes 9437188
  121.3 3.0 %copy-start.1 = (f32[48,128,128]{2,1,0:T(8,128)S(1)}, f32[48,128,128]{2,1,0:T(8,128)}, u32[]{:S(2)}) copy-start(f32[48,128,128]{2,1,0:T(8,128)} %get-tuple-element.13) | copy-start | bytes 9437188
  124.3 3.0 %copy-start = (f32[48,128,128]{2,1,0:T(8,128)S(1)}, f32[48,128,128]{2,1,0:T(8,128)}, u32[]{:S(2)}) copy-start(f32[48,128,128]{2,1,0:T(8,128)} %get-tuple-element.14) | copy-start | bytes 9437188
where the time goes:
time: 129 us
  Pallas kernels  114 us (88%)
  local copies, waits for them, and re-layouts  14.8 us (11%)
    pallas_call x1, Pallas kernels, local(): pl.pallas_call(functools.partial(kernel, n, ni, nj, sizes), out_shape=[ja...  114 us
    unnamed x13, local copies, waits for them, and re-layouts  14.8 us

commit v1 on v0

--- a/solution.py
+++ b/solution.py
@@ -11,7 +11,7 @@
 STIFF = 30.0
 PAD = 8
 ROWS = 16
-UNROLL = 4
+UNROLL = 24
 
 
 def roll(value, shift):
@@ -26,6 +26,7 @@
            row_out, row_in, col_out, col_in, z_out, z_in,
            load_sem, row_send, row_recv, col_send, col_recv, z_send, z_recv):
     nx, ny, nz = sizes
+    unroll = max(u for u in range(1, UNROLL + 1) if n % u == 0)
     ix, iy, iz = lax.axis_index("gx"), lax.axis_index("gy"), lax.axis_index("gz")
     xs = (lax.rem(ix + nx - 1, nx), lax.rem(ix + 1, nx))
     ys = (lax.rem(iy + ny - 1, ny), lax.rem(iy + 1, ny))
@@ -95,12 +96,12 @@
             zero = jnp.zeros((ROWS, nj), jnp.float32)
 
             def group(q, packs):
-                for e in range(UNROLL):
-                    k = q * UNROLL + e
+                for e in range(unroll):
+                    k = q * unroll + e
                     packs = packed(load_level(k, r0), k, packs)
                 return packs
 
-            packs = lax.fori_loop(0, n // UNROLL, group, (zero, zero))
+            packs = lax.fori_loop(0, n // unroll, group, (zero, zero))
             for t in range(2):
                 col_out[slot, t, pl.ds(r0, ROWS), :] = packs[t]
 
@@ -182,13 +183,13 @@
 
             zero = jnp.zeros((ROWS, nj), jnp.float32)
             carry = (zero, zero, (zero, zero, zero + 1.0))
-            carry = steps(range(UNROLL), carry)
+            carry = steps(range(unroll), carry)
             planes_lo = press[0, rows, :]
 
             def group(q, carry):
-                return steps([q * UNROLL + e for e in range(UNROLL)], carry)
-
-            older, newer, state = lax.fori_loop(1, n // UNROLL, group, carry)
+                return steps([q * unroll + e for e in range(unroll)], carry)
+
+            older, newer, state = lax.fori_loop(1, n // unroll, group, carry)
             y, dn, _ = sweep(n - 1, zero, older, state)
             z_out[it, 0, rows, :] = y
             z_out[it, 1, rows, :] = dn
@@ -283,12 +284,12 @@
 
             top = bounds[3, rows, :]
             carry = (bounds[0, rows, :], bounds[1, rows, :], zero, top, (zero, zero))
-            carry = steps([n - 1 - e for e in range(UNROLL)], carry)
+            carry = steps([n - 1 - e for e in range(unroll)], carry)
 
             def group(q, carry):
-                return steps([n - 1 - q * UNROLL - e for e in range(UNROLL)], carry)
-
-            _, _, older, newer, packs = lax.fori_loop(1, n // UNROLL, group, carry)
+                return steps([n - 1 - q * unroll - e for e in range(unroll)], carry)
+
+            _, _, older, newer, packs = lax.fori_loop(1, n // unroll, group, carry)
             packs = finish(0, older, bounds[2, rows, :], packs)
             if not last:
                 for t in range(2):
@@ -306,8 +307,8 @@
                 right = right + col_in[it, 1, rows, :]
 
             def group(q, carry):
-                for e in range(UNROLL):
-                    k = q * UNROLL + e
+                for e in range(unroll):
+                    k = q * unroll + e
                     at = pl.ds(PAD + r0, ROWS)
                     p = psum[k, at, :]
                     east[k, rows, :] = up[k, at, :] - 0.25 * (
@@ -317,7 +318,7 @@
                     north[k, rows, :] = north[k, rows, :] - 0.25 * (high - low)
                 return carry
 
-            lax.fori_loop(0, n // UNROLL, group, 0)
+            lax.fori_loop(0, n // unroll, group, 0)
 
         strips(body)
 
@@ -356,7 +357,7 @@
     plane = pltpu.VMEM((ni, nj), f32)
     return pl.pallas_call(
         functools.partial(kernel, n, ni, nj, sizes),
-        out_shape=[jax.ShapeDtypeStruct((n, ni, nj), f32)] * 5,
+        out_shape=[pltpu.VMEM((n, ni, nj), f32)] * 5,
         in_specs=[pl.BlockSpec(memory_space=pl.ANY)] * 5 + [pl.BlockSpec(memory_space=pltpu.VMEM)],
         out_specs=[pl.BlockSpec(memory_space=pltpu.VMEM)] * 5,
         scratch_shapes=[
@@ -378,7 +379,7 @@
             pltpu.SemaphoreType.DMA((ITERS, nz - 1)),
         ],
         compiler_params=pltpu.CompilerParams(
-            collective_id=0, has_side_effects=True, vmem_limit_bytes=60 * 1024 * 1024),
+            collective_id=0, has_side_effects=True, vmem_limit_bytes=40 * 1024 * 1024),
     )(east, north, vert, geo, press, mass)
 
 

time: 129 us -> 63.7 us (0.49)
  Pallas kernels: 114 us -> 54.5 us
  local copies, waits for them, and re-layouts: 14.8 us -> 8.32 us
    pallas_call x1, Pallas kernels: 114 us -> 54.5 us  [local(): pl.pallas_call(functools.partial(kernel, n, ni, nj, sizes), out_shape=[pl...]
    unnamed x13 -> x5, local copies, waits for them, and re-layouts: 14.8 us -> 8.32 us
where the time goes in v1:
time: 63.7 us; the launch traced here: 63.5 us
  Pallas kernels  54.5 us (86%)
  local copies, waits for them, and re-layouts  8.32 us (13%)
  between operations  0.64 us (1%)
    pallas_call x1, Pallas kernels, local(): pl.pallas_call(functools.partial(kernel, n, ni, nj, sizes), out_shape=[pl...  54.5 us
    unnamed x5, local copies, waits for them, and re-layouts  8.32 us

profile of v1, /device:TPU:0, one launch (start us, length us, event | category | flops | bytes accessed | tf_op | source)
XLA Modules:
  0.0 63.5 jit_solution(11698669523768631208)
XLA Ops:
  0.6 54.5 %shard_map.101 = (f32[48,128,128]{2,1,0:T(8,128)S(1)}, f32[48,128,128]{2,1,0:T(8,128)S(1)}, f32[48,128,128]{2,1,0:T(8,128)S(1)}, f32[48,128,128]{2,1,0:T(8,128)S(1)}, f32[48,128,128]{2,1,0:T(8,128)S(1)}) custom-call(f32[48,128,128]{2,1,0:T(8,128)} %east_in.1, f32[48,128,128]{2,1,0:T(8,128)} %north_in.1, f32[48,128,128]{2,1,0:T(8,128)} %vert_in.1, ...), custom_call_target="tpu_custom_call" | custom-call | tf_op jit(solution)/shard_map/pallas_call | solution.py:358
  55.2 1.7 %copy.16 = f32[48,128,128]{2,1,0:T(8,128)} copy(f32[48,128,128]{2,1,0:T(8,128)S(1)} %get-tuple-element.5) | data formatting | bytes 6291456
  56.9 1.7 %copy.17 = f32[48,128,128]{2,1,0:T(8,128)} copy(f32[48,128,128]{2,1,0:T(8,128)S(1)} %get-tuple-element.6) | data formatting | bytes 6291456
  58.5 1.7 %copy.18 = f32[48,128,128]{2,1,0:T(8,128)} copy(f32[48,128,128]{2,1,0:T(8,128)S(1)} %get-tuple-element.7) | data formatting | bytes 6291456
  60.2 1.7 %copy.19 = f32[48,128,128]{2,1,0:T(8,128)} copy(f32[48,128,128]{2,1,0:T(8,128)S(1)} %get-tuple-element.8) | data formatting | bytes 6291456
  61.8 1.7 %copy.20 = f32[48,128,128]{2,1,0:T(8,128)} copy(f32[48,128,128]{2,1,0:T(8,128)S(1)} %get-tuple-element.9) | data formatting | bytes 6291456

commit v2 on v1

--- a/solution.py
+++ b/solution.py
@@ -11,6 +11,7 @@
 STIFF = 30.0
 PAD = 8
 ROWS = 16
+PARTS = 2
 UNROLL = 24
 
 
@@ -26,7 +27,7 @@
            row_out, row_in, col_out, col_in, z_out, z_in,
            load_sem, row_send, row_recv, col_send, col_recv, z_send, z_recv):
     nx, ny, nz = sizes
-    unroll = max(u for u in range(1, UNROLL + 1) if n % u == 0)
+    unroll = max(u for u in range(2, UNROLL + 1) if n % u == 0 and u % 2 == 0)
     ix, iy, iz = lax.axis_index("gx"), lax.axis_index("gy"), lax.axis_index("gz")
     xs = (lax.rem(ix + nx - 1, nx), lax.rem(ix + 1, nx))
     ys = (lax.rem(iy + ny - 1, ny), lax.rem(iy + 1, ny))
@@ -55,20 +56,30 @@
             send_sem=row_send.at[slot, t], recv_sem=row_recv.at[slot, 1 - t],
             device_id={"gx": xs[t]})
 
-    def col_copy(slot, t):
+    span = ni // PARTS
+
+    def part_rows(h):
+        return pl.ds(pl.multiple_of(h * span, span), span)
+
+    def col_copy(slot, t, h):
         return pltpu.make_async_remote_copy(
-            src_ref=col_out.at[slot, t], dst_ref=col_in.at[slot, 1 - t],
-            send_sem=col_send.at[slot, t], recv_sem=col_recv.at[slot, 1 - t],
+            src_ref=col_out.at[slot, t, part_rows(h), :], dst_ref=col_in.at[slot, 1 - t, part_rows(h), :],
+            send_sem=col_send.at[slot, t, h], recv_sem=col_recv.at[slot, 1 - t, h],
             device_id={"gy": ys[t]})
 
-    def z_copy(slot, d):
+    def z_copy(slot, d, h):
         return pltpu.make_async_remote_copy(
-            src_ref=z_out.at[slot], dst_ref=z_in.at[slot, d - 1],
-            send_sem=z_send.at[slot, d - 1], recv_sem=z_recv.at[slot, d - 1],
+            src_ref=z_out.at[slot, :, part_rows(h), :], dst_ref=z_in.at[slot, d - 1, :, part_rows(h), :],
+            send_sem=z_send.at[slot, d - 1, h], recv_sem=z_recv.at[slot, d - 1, h],
             device_id={"gz": lax.rem(iz + d, nz)})
 
     lane = lax.broadcasted_iota(jnp.int32, (ROWS, nj), 1)
     pair = lane // 2
+
+    def merged(left, right, width):
+        left, right = roll(left, width), roll(right, nj - width)
+        even = pair % 2 == 0
+        return jnp.where(even, right, left), jnp.where(even, left, right)
 
     def send_rows(slot, ref):
         row_out[slot, 0] = ref[:, PAD : PAD + 2, :]
@@ -86,10 +97,13 @@
         turned = roll(value, 2 * k + 2)
         return (jnp.where(pair == k + 1, turned, packs[0]), jnp.where(pair == k, turned, packs[1]))
 
-    def strips(body):
-        @pl.loop(0, ni // ROWS)
+    def strips(body, h=None):
+        count = (ni if h is None else span) // ROWS
+        first = 0 if h is None else h * count
+
+        @pl.loop(0, count)
         def _(s):
-            body(pl.multiple_of(s * ROWS, ROWS))
+            body(pl.multiple_of((first + s) * ROWS, ROWS))
 
     def send_cols(slot, load_level):
         def body(r0):
@@ -106,8 +120,9 @@
                 col_out[slot, t, pl.ds(r0, ROWS), :] = packs[t]
 
         strips(body)
-        for t in range(2):
-            col_copy(slot, t).start()
+        for h in range(PARTS):
+            for t in range(2):
+                col_copy(slot, t, h).start()
 
     loads[0].wait()
     send_rows(0, pp)
@@ -130,29 +145,33 @@
     recv_rows(ITERS, up)
     for slot in (0, ITERS):
         for t in range(2):
-            col_copy(slot, t).wait()
+            for h in range(PARTS):
+                col_copy(slot, t, h).wait()
     loads[3].wait()
     loads[4].wait()
 
-    def pass_one(it):
+    def pass_one(it, h):
         def body(r0):
             rows = pl.ds(r0, ROWS)
             m, mu, c = mass[rows, :], mu_s[rows, :], c_s[rows, :]
             weak, strong = 0.05 * m, 0.2 * m
             left, right = col_in[it, 0, rows, :], col_in[it, 1, rows, :]
+            ends = merged(left, right, 2)
             if it == 0:
-                vleft, vright = col_in[ITERS, 0, rows, :], col_in[ITERS, 1, rows, :]
-
-            def star(k):
+                vends = merged(col_in[ITERS, 0, rows, :], col_in[ITERS, 1, rows, :], 1)
+
+            def star(k, parity):
+                end = roll(ends[parity], nj - 2 - 2 * k)
                 at = pl.ds(PAD + r0, ROWS)
                 p = pp[k, at, :]
-                low = jnp.where(lane < 2, roll(left, (2 * nj - 2 * k) if isinstance(k, int) else nj - 2 * k), roll(p, 2))
-                high = jnp.where(lane >= nj - 2, roll(right, nj - 4 - 2 * k), roll(p, nj - 2))
+                low = jnp.where(lane < 2, end, roll(p, 2))
+                high = jnp.where(lane >= nj - 2, end, roll(p, nj - 2))
                 total = (pp[k, pl.ds(PAD + r0 + 2, ROWS), :] + pp[k, pl.ds(PAD + r0 - 2, ROWS), :]) + (low + high) - 4.0 * p
                 if it == 0:
                     v = north[k, rows, :]
-                    vlow = jnp.where(lane < 1, roll(vleft, nj - 1 - 2 * k), roll(v, 1))
-                    vhigh = jnp.where(lane >= nj - 1, roll(vright, nj - 3 - 2 * k), roll(v, nj - 1))
+                    vend = roll(vends[parity], nj - 2 - 2 * k)
+                    vlow = jnp.where(lane < 1, vend, roll(v, 1))
+                    vhigh = jnp.where(lane >= nj - 1, vend, roll(v, nj - 1))
                     d = strong * (up[k, pl.ds(PAD + r0 + 1, ROWS), :] - up[k, pl.ds(PAD + r0 - 1, ROWS), :] + (vhigh - vlow))
                     psum[k, at, :] = p
                 else:
@@ -174,8 +193,8 @@
 
             def steps(ks, carry):
                 older, newer, state = carry
-                for k in ks:
-                    ps = star(k)
+                for e, k in enumerate(ks):
+                    ps = star(k, e % 2)
                     if not (isinstance(k, int) and k == 0):
                         state = sweep(k - 1, ps, older, state)
                     older, newer = newer, ps
@@ -196,9 +215,9 @@
             z_out[it, 2, rows, :] = c * planes_lo
             z_out[it, 3, rows, :] = c * newer
 
-        strips(body)
-
-    def interface(it):
+        strips(body, h)
+
+    def interface(it, h):
         def body(r0):
             rows = pl.ds(r0, ROWS)
             mu, logmu, kappa, inv = mu_s[rows, :], planes[0, rows, :], planes[1, rows, :], planes[2, rows, :]
@@ -250,9 +269,9 @@
             bounds[0, rows, :] = kappa * mu * z_out[it, 0, rows, :] + beta
             bounds[1, rows, :] = alpha * power(n)
 
-        strips(body)
-
-    def pass_two(it):
+        strips(body, h)
+
+    def pass_two(it, h):
         last = it == ITERS - 1
 
         def body(r0):
@@ -295,7 +314,7 @@
                 for t in range(2):
                     col_out[it + 1, t, rows, :] = packs[t]
 
-        strips(body)
+        strips(body, h)
 
     def winds():
         def body(r0):
@@ -306,15 +325,18 @@
                 left = left + col_in[it, 0, rows, :]
                 right = right + col_in[it, 1, rows, :]
 
+            ends = merged(left, right, 1)
+
             def group(q, carry):
                 for e in range(unroll):
                     k = q * unroll + e
+                    end = roll(ends[e % 2], nj - 2 - 2 * k)
                     at = pl.ds(PAD + r0, ROWS)
                     p = psum[k, at, :]
                     east[k, rows, :] = up[k, at, :] - 0.25 * (
                         psum[k, pl.ds(PAD + r0 + 1, ROWS), :] - psum[k, pl.ds(PAD + r0 - 1, ROWS), :])
-                    low = jnp.where(lane < 1, roll(left, nj - 1 - 2 * k), roll(p, 1))
-                    high = jnp.where(lane >= nj - 1, roll(right, nj - 3 - 2 * k), roll(p, nj - 1))
+                    low = jnp.where(lane < 1, end, roll(p, 1))
+                    high = jnp.where(lane >= nj - 1, end, roll(p, nj - 1))
                     north[k, rows, :] = north[k, rows, :] - 0.25 * (high - low)
                 return carry
 
@@ -325,11 +347,16 @@
     for it in range(ITERS):
         if it > 0:
             recv_rows(it, pp)
-            for t in range(2):
-                col_copy(it, t).wait()
-        pass_one(it)
-        for d in range(1, nz):
-            z_copy(it, d).start()
+
+        @pl.loop(0, PARTS)
+        def _(h, it=it):
+            if it > 0:
+                for t in range(2):
+                    col_copy(it, t, h).wait()
+            pass_one(it, h)
+            for d in range(1, nz):
+                z_copy(it, d, h).start()
+
         if it == ITERS - 1:
             for t, at in ((0, PAD - 2), (1, PAD + ni)):
                 total = row_in[0, t]
@@ -337,14 +364,19 @@
                     total = total + row_in[slot, t]
                 psum[:, at : at + 2, :] = total
             winds()
-        for d in range(1, nz):
-            z_copy(it, d).wait()
-        interface(it)
-        pass_two(it)
+
+        @pl.loop(0, PARTS)
+        def _(h, it=it):
+            for d in range(1, nz):
+                z_copy(it, d, h).wait()
+            interface(it, h)
+            pass_two(it, h)
+            if it < ITERS - 1:
+                for t in range(2):
+                    col_copy(it + 1, t, h).start()
+
         if it < ITERS - 1:
             send_rows(it + 1, pp)
-            for t in range(2):
-                col_copy(it + 1, t).start()
 
 
 def local(sizes, east, north, vert, geo, press, mass):
@@ -373,10 +405,10 @@
             pltpu.SemaphoreType.DMA((5,)),
             pltpu.SemaphoreType.DMA((slots, 2)),
             pltpu.SemaphoreType.DMA((slots, 2)),
-            pltpu.SemaphoreType.DMA((slots, 2)),
-            pltpu.SemaphoreType.DMA((slots, 2)),
-            pltpu.SemaphoreType.DMA((ITERS, nz - 1)),
-            pltpu.SemaphoreType.DMA((ITERS, nz - 1)),
+            pltpu.SemaphoreType.DMA((slots, 2, PARTS)),
+            pltpu.SemaphoreType.DMA((slots, 2, PARTS)),
+            pltpu.SemaphoreType.DMA((ITERS, nz - 1, PARTS)),
+            pltpu.SemaphoreType.DMA((ITERS, nz - 1, PARTS)),
         ],
         compiler_params=pltpu.CompilerParams(
             collective_id=0, has_side_effects=True, vmem_limit_bytes=40 * 1024 * 1024),

time: 63.7 us -> 58.9 us (0.925)
  Pallas kernels: 54.5 us -> 49.8 us
    pallas_call x1, Pallas kernels: 54.5 us -> 49.8 us  [local(): pl.pallas_call(functools.partial(kernel, n, ni, nj, sizes), out_shape=[pl...]
where the time goes in v2:
time: 58.9 us; the launch traced here: 58.8 us
  Pallas kernels  49.8 us (85%)
  local copies, waits for them, and re-layouts  8.32 us (14%)
  between operations  0.64 us (1%)
    pallas_call x1, Pallas kernels, local(): pl.pallas_call(functools.partial(kernel, n, ni, nj, sizes), out_shape=[pl...  49.8 us
    unnamed x5, local copies, waits for them, and re-layouts  8.32 us

profile of v2, /device:TPU:0, one launch (start us, length us, event | category | flops | bytes accessed | tf_op | source)
XLA Modules:
  0.0 58.8 jit_solution(9270031546268181369)
XLA Ops:
  0.6 49.8 %shard_map.101 = (f32[48,128,128]{2,1,0:T(8,128)S(1)}, f32[48,128,128]{2,1,0:T(8,128)S(1)}, f32[48,128,128]{2,1,0:T(8,128)S(1)}, f32[48,128,128]{2,1,0:T(8,128)S(1)}, f32[48,128,128]{2,1,0:T(8,128)S(1)}) custom-call(f32[48,128,128]{2,1,0:T(8,128)} %east_in.1, f32[48,128,128]{2,1,0:T(8,128)} %north_in.1, f32[48,128,128]{2,1,0:T(8,128)} %vert_in.1, ...), custom_call_target="tpu_custom_call" | custom-call | tf_op jit(solution)/shard_map/pallas_call | solution.py:390
  50.4 1.7 %copy.16 = f32[48,128,128]{2,1,0:T(8,128)} copy(f32[48,128,128]{2,1,0:T(8,128)S(1)} %get-tuple-element.5) | data formatting | bytes 6291456
  52.1 1.7 %copy.17 = f32[48,128,128]{2,1,0:T(8,128)} copy(f32[48,128,128]{2,1,0:T(8,128)S(1)} %get-tuple-element.6) | data formatting | bytes 6291456
  53.8 1.7 %copy.18 = f32[48,128,128]{2,1,0:T(8,128)} copy(f32[48,128,128]{2,1,0:T(8,128)S(1)} %get-tuple-element.7) | data formatting | bytes 6291456
  55.4 1.7 %copy.19 = f32[48,128,128]{2,1,0:T(8,128)} copy(f32[48,128,128]{2,1,0:T(8,128)S(1)} %get-tuple-element.8) | data formatting | bytes 6291456
  57.1 1.7 %copy.20 = f32[48,128,128]{2,1,0:T(8,128)} copy(f32[48,128,128]{2,1,0:T(8,128)S(1)} %get-tuple-element.9) | data formatting | bytes 6291456
